TPU v7x, 32 devices: a whole 2x2x4 slice. The times are simulated.
32 devices in a mesh: outer: 4 (over z), inner: 2 (over x), head: 4 (over y, core).
Axes of the slice: x: 2, y: 2, z: 4, core: 2. Of those that a mesh axis runs over, the one named last changes fastest.
Arguments:
- stored_query_rows: bfloat16 [2048, 32, 128], P(('outer', 'inner'), 'head'), may hold values from -12 to 12
- stored_key_rows: bfloat16 [2048, 8, 128], P(('outer', 'inner'), 'head'), may hold values from -12 to 12
- stored_value_rows: bfloat16 [2048, 8, 128], P(('outer', 'inner'), 'head'), may hold values from -6 to 6
- span_order: int32 [16], replicated, may hold values from 0 to 15, each once
Outputs:
- attended: bfloat16 [2048, 32, 128], P(('outer', 'inner'), 'head')
Inputs may be any that keep to these rules, and one draw needn't show every extreme that they name: `span_order`: a permutation of the sequence's 16 blocks of 128 tokens.
All inputs are finite; a program needn't handle non-finite values.
Results may differ from a plain program's by a relative error of at most 0.0075.
Values may be sent and summed in bfloat16 or wider, within the bound.
A program may use at most 128 MiB of HBM per device.

v0:
```python
import functools
import math

import jax
import jax.numpy as jnp
from jax import lax
from jax.experimental import pallas as pl
from jax.experimental.pallas import tpu as pltpu
from jax.sharding import PartitionSpec as P

MESH = pl.DeviceIdType.MESH
MASKED = -1e30
TILE = 256
CHUNKS = 2


def kernel(
    n_outer,
    n_inner,
    heads,
    span_ref,
    q_ref,
    kv_ref,
    o_ref,
    wide_ref,
    held,
    top_ref,
    sum_ref,
    acc_ref,
    send_up,
    send_down,
    send_across,
    recv_sem,
):
    rows, width = q_ref.shape
    kv_rows = kv_ref.shape[0]
    pair = kv_ref.shape[1] // 2
    span = kv_rows // 2
    chunk = kv_rows // CHUNKS
    tiles = rows // TILE
    factor = math.log2(math.e) / math.sqrt(width)
    outer = lax.axis_index("outer")
    inner = lax.axis_index("inner")

    barrier = pltpu.get_barrier_semaphore()

    @pl.when(outer > 0)
    def _():
        pl.semaphore_signal(barrier, inc=1, device_id={"outer": outer - 1}, device_id_type=MESH)

    @pl.when(outer < n_outer - 1)
    def _():
        pl.semaphore_signal(barrier, inc=1, device_id={"outer": outer + 1}, device_id_type=MESH)

    for step in range(1, n_inner):
        peer = lax.rem(inner + step, n_inner)
        pl.semaphore_signal(barrier, inc=1, device_id={"inner": peer}, device_id_type=MESH)

    ends = jnp.minimum(outer, 1) + jnp.minimum(n_outer - 1 - outer, 1)
    pl.semaphore_wait(barrier, n_inner - 1 + ends)

    def copy_of(source, src_outer, src_inner, part, send_sem, target):
        return pltpu.make_async_remote_copy(
            src_ref=source.at[pl.ds(part * chunk, chunk)],
            dst_ref=held.at[src_outer, src_inner, pl.ds(part * chunk, chunk)],
            send_sem=send_sem,
            recv_sem=recv_sem.at[src_outer, src_inner, part],
            device_id=target,
            device_id_type=MESH,
        )

    def up(source, src_outer, part):
        return copy_of(
            source, src_outer, inner, part, send_up.at[src_outer, part], {"outer": outer + 1}
        )

    def down(source, src_outer, part):
        return copy_of(
            source, src_outer, inner, part, send_down.at[src_outer, part], {"outer": outer - 1}
        )

    def across(source, src_outer, part, step):
        peer = lax.rem(inner + step, n_inner)
        return copy_of(
            source,
            src_outer,
            inner,
            part,
            send_across.at[src_outer, part, step - 1],
            {"inner": peer},
        )

    def pass_on(source, src_outer, part, act):
        @pl.when(jnp.logical_and(src_outer <= outer, outer < n_outer - 1))
        def _():
            act(up(source, src_outer, part))

        @pl.when(jnp.logical_and(src_outer >= outer, outer > 0))
        def _():
            act(down(source, src_outer, part))

        for step in range(1, n_inner):
            act(across(source, src_outer, part, step))

    def arrived(src_outer, src_inner, part):
        place = held.at[src_outer, src_inner, pl.ds(part * chunk, chunk)]
        pltpu.make_async_remote_copy(
            src_ref=place,
            dst_ref=place,
            send_sem=recv_sem.at[src_outer, src_inner, part],
            recv_sem=recv_sem.at[src_outer, src_inner, part],
            device_id={"inner": lax.rem(inner + 1, n_inner)},
            device_id_type=MESH,
        ).wait_recv()

    for part in range(CHUNKS):
        pass_on(kv_ref, outer, part, lambda copy: copy.start())

    row_head = lax.rem(lax.broadcasted_iota(jnp.int32, (TILE, width), 0), heads)
    first_head = row_head < heads // 2
    keep_first = jnp.where(first_head, 1.0, 0.0).astype(q_ref.dtype)
    keep_second = jnp.where(first_head, 0.0, 1.0).astype(q_ref.dtype)
    here = (outer * n_inner + inner) * 2
    lane = lax.broadcasted_iota(jnp.int32, (TILE, kv_rows), 1)

    def attend(block, value):
        pv = jnp.dot(block.astype(jnp.bfloat16), value, preferred_element_type=jnp.float32)
        return jnp.where(first_head, pv[:, :width], pv[:, width:])

    def scores_of(wide, key):
        return lax.dot_general(
            wide, key, (((1,), (1,)), ((), ())), preferred_element_type=jnp.float32
        )

    def own_tile(index, carry):
        at = pl.ds(pl.multiple_of(index * TILE, TILE), TILE)
        query = q_ref[at, :]
        wide = jnp.concatenate([query * keep_first, query * keep_second], axis=1)
        wide_ref[at, :] = wide
        scores = scores_of(wide, kv_ref[:, :pair])
        q_block = index // (tiles // 2)
        q_anchor = span_ref[here + q_block]
        row = lax.broadcasted_iota(jnp.int32, (TILE, kv_rows), 0)
        q_offset = (row + (index - q_block * (tiles // 2)) * TILE) // heads
        anchor = jnp.where(lane < span, span_ref[here], span_ref[here + 1])
        key_pos = anchor * span + lax.rem(lane, span)
        allowed = key_pos <= q_anchor * span + q_offset
        scores = jnp.where(allowed, scores, MASKED)
        top = jnp.max(scores, axis=1, keepdims=True)
        weights = jnp.exp2((scores - top) * factor)
        top_ref[at, :] = jnp.broadcast_to(top, (TILE, width))
        sum_ref[at, :] = weights[:, :width] + weights[:, width:]
        acc_ref[at, :] = attend(weights, kv_ref[:, pair:])
        return carry

    lax.fori_loop(0, tiles, own_tile, 0)

    def visit(src_outer, src_inner):
        base = (src_outer * n_inner + src_inner) * 2
        anchors = [span_ref[base], span_ref[base + 1]]
        place = held.at[src_outer, src_inner]

        def tile(index, carry):
            at = pl.ds(pl.multiple_of(index * TILE, TILE), TILE)
            q_anchor = span_ref[here + index // (tiles // 2)]
            bias = [jnp.where(anchor < q_anchor, 0.0, MASKED) for anchor in anchors]
            scores = scores_of(wide_ref[at, :], place[:, :pair])
            left = scores[:, :width] + bias[0]
            right = scores[:, width:] + bias[1]
            old = top_ref[at, :]
            top = jnp.maximum(old, jnp.max(jnp.maximum(left, right), axis=1, keepdims=True))
            rescale = jnp.exp2((old - top) * factor)
            left = jnp.exp2((left - top) * factor)
            right = jnp.exp2((right - top) * factor)
            top_ref[at, :] = top
            sum_ref[at, :] = sum_ref[at, :] * rescale + (left + right)
            weights = jnp.concatenate([left, right], axis=1)
            acc_ref[at, :] = acc_ref[at, :] * rescale + attend(weights, place[:, pair:])
            return carry

        lax.fori_loop(0, tiles, tile, 0, unroll=2)

    below = jnp.minimum(outer, n_outer - 1 - outer)

    def nth(step):
        paired = step <= 2 * below
        distance = jnp.where(paired, (step + 1) // 2, step - below)
        upward = jnp.where(
            paired, lax.rem(step, 2) == 0, outer < n_outer - 1 - outer
        )
        return jnp.where(upward, outer + distance, outer - distance)

    def from_inner(src_outer):
        for step in range(1, n_inner):
            src_inner = lax.rem(inner + step, n_inner)
            for part in range(CHUNKS):
                arrived(src_outer, src_inner, part)
            visit(src_outer, src_inner)

    def line_step(step, carry):
        src_outer = nth(step)
        for part in range(CHUNKS):
            arrived(src_outer, inner, part)
            pass_on(held.at[src_outer, inner], src_outer, part, lambda copy: copy.start())
        from_inner(nth(step - 1))
        visit(src_outer, inner)
        return carry

    lax.fori_loop(1, n_outer, line_step, 0)
    from_inner(nth(n_outer - 1))

    def finish(index, carry):
        at = pl.ds(pl.multiple_of(index * TILE, TILE), TILE)
        total = jnp.sum(sum_ref[at, :], axis=1, keepdims=True)
        o_ref[at, :] = (acc_ref[at, :] / total).astype(o_ref.dtype)
        return carry

    lax.fori_loop(0, tiles, finish, 0)

    def settle(src_outer, carry):
        for part in range(CHUNKS):
            pass_on(kv_ref, src_outer, part, lambda copy: copy.wait_send())
        return carry

    lax.fori_loop(0, n_outer, settle, 0)


def solution(mesh):
    n_outer, n_inner = mesh.shape["outer"], mesh.shape["inner"]

    def body(query, key, value, span_order):
        kv_rows, groups, width = key.shape
        heads = query.shape[1]
        rows = query.shape[0] * heads
        kv = jnp.concatenate(
            [key.reshape(kv_rows, groups * width), value.reshape(kv_rows, groups * width)], axis=1
        )
        vmem = pl.BlockSpec(memory_space=pltpu.VMEM)
        out = pl.pallas_call(
            functools.partial(kernel, n_outer, n_inner, heads),
            out_shape=jax.ShapeDtypeStruct((rows, width), jnp.bfloat16),
            in_specs=[pl.BlockSpec(memory_space=pltpu.SMEM), vmem, vmem],
            out_specs=vmem,
            scratch_shapes=[
                pltpu.VMEM((rows, groups * width), jnp.bfloat16),
                pltpu.VMEM((n_outer, n_inner) + kv.shape, jnp.bfloat16),
                pltpu.VMEM((rows, width), jnp.float32),
                pltpu.VMEM((rows, width), jnp.float32),
                pltpu.VMEM((rows, width), jnp.float32),
                pltpu.SemaphoreType.DMA((n_outer, CHUNKS)),
                pltpu.SemaphoreType.DMA((n_outer, CHUNKS)),
                pltpu.SemaphoreType.DMA((n_outer, CHUNKS, max(n_inner - 1, 1))),
                pltpu.SemaphoreType.DMA((n_outer, n_inner, CHUNKS)),
            ],
            compiler_params=pltpu.CompilerParams(
                collective_id=0, has_side_effects=True, vmem_limit_bytes=48 * 1024 * 1024
            ),
        )(span_order, query.reshape(rows, width), kv)
        return out.reshape(query.shape)

    placed = P(("outer", "inner"), "head", None)
    return jax.shard_map(
        body,
        mesh=mesh,
        in_specs=(placed, placed, placed, P()),
        out_specs=placed,
        check_vma=False,
    )
```

profile of v0, /device:TPU:0, one launch (start us, length us, event | category | flops | bytes accessed | tf_op | source)
XLA Modules:
  0.0 42.9 jit_solution(3872708487302214140)
XLA Ops:
  0.0 0.0 copy-start
  0.0 1.1 %copy_bitcast_fusion = (bf16[256,256]{1,0:T(8,128)(2,1)S(1)}, bf16[256,256]{1,0:T(8,128)(2,1)S(1)}) fusion(bf16[32,8,2,128]{3,2,1,0:T(2,128)(2,1)} %bitcast.10, bf16[32,8,2,128]{3,2,1,0:T(2,128)(2,1)} %bitcast.11), kind=kLoop, calls=%fused_computation.1 | loop fusion | bytes 524288 | tf_op jit(solution)/shard_map/reshape | solution.py:236
  1.1 0.0 copy-start.1
  1.1 0.1 copy-done
  1.2 0.6 %copy-done.1 = s32[16]{0:T(128)S(1)} copy-done((s32[16]{0:T(128)S(1)}, s32[16]{0:T(128)}, u32[]{:S(2)}) %copy-start.1) | copy-done | bytes 88
  1.7 40.3 %shard_map.46 = bf16[2048,128]{1,0:T(8,128)(2,1)S(1)} custom-call(s32[16]{0:T(128)S(1)} %copy-done.1, bf16[2048,128]{1,0:T(8,128)(2,1)S(1)} %bitcast.9, bf16[256,512]{1,0:T(8,128)(2,1)S(1)} %pad_maximum_fusion.kv_ref), custom_call_target="tpu_custom_call" | custom-call | tf_op jit(solution)/shard_map/pallas_call | solution.py:239
  42.1 0.8 %copy.10 = bf16[256,8,128]{2,1,0:T(8,128)(2,1)} copy(bf16[256,8,128]{2,1,0:T(8,128)(2,1)S(1)} %bitcast.8) | data formatting | bytes 1048576
  (1 shorter events, 0.0 us)
Async XLA Ops:
  0.0 1.2 %copy-start = (bf16[256,8,128]{2,1,0:T(8,128)(2,1)S(1)}, bf16[256,8,128]{2,1,0:T(8,128)(2,1)}, u32[]{:S(2)}) copy-start(bf16[256,8,128]{2,1,0:T(8,128)(2,1)} %param.4) | copy-start | bytes 1572868
  1.1 0.7 %copy-start.1 = (s32[16]{0:T(128)S(1)}, s32[16]{0:T(128)}, u32[]{:S(2)}) copy-start(s32[16]{0:T(128)} %span_ref.1) | copy-start | bytes 196
where the time goes:
time: 43 us; the launch traced here: 42.9 us
  Pallas kernels  40.3 us (94%)
  local copies, waits for them, and re-layouts  2.5 us (6%)
    pallas_call x1, Pallas kernels, body(): pl.pallas_call(functools.partial(kernel, n_outer, n_inner, heads), out_sh...  40.3 us
    unnamed x5, local copies, waits for them, and re-layouts  1.44 us
    reshape x1, local copies, waits for them, and re-layouts, body(): value.reshape(kv_rows, groups * width)  1.06 us

commit v1 on v0

--- a/solution.py
+++ b/solution.py
@@ -10,7 +10,7 @@
 
 MESH = pl.DeviceIdType.MESH
 MASKED = -1e30
-TILE = 256
+TILE = 512
 CHUNKS = 2
 
 
@@ -132,53 +132,67 @@
             wide, key, (((1,), (1,)), ((), ())), preferred_element_type=jnp.float32
         )
 
-    def own_tile(index, carry):
-        at = pl.ds(pl.multiple_of(index * TILE, TILE), TILE)
-        query = q_ref[at, :]
+    def at(index):
+        return pl.ds(index * TILE, TILE)
+
+    def own_scores(index):
+        query = q_ref[at(index), :]
         wide = jnp.concatenate([query * keep_first, query * keep_second], axis=1)
-        wide_ref[at, :] = wide
-        scores = scores_of(wide, kv_ref[:, :pair])
-        q_block = index // (tiles // 2)
-        q_anchor = span_ref[here + q_block]
+        wide_ref[at(index), :] = wide
+        return scores_of(wide, kv_ref[:, :pair])
+
+    def visit_own():
         row = lax.broadcasted_iota(jnp.int32, (TILE, kv_rows), 0)
-        q_offset = (row + (index - q_block * (tiles // 2)) * TILE) // heads
         anchor = jnp.where(lane < span, span_ref[here], span_ref[here + 1])
-        key_pos = anchor * span + lax.rem(lane, span)
-        allowed = key_pos <= q_anchor * span + q_offset
-        scores = jnp.where(allowed, scores, MASKED)
-        top = jnp.max(scores, axis=1, keepdims=True)
-        weights = jnp.exp2((scores - top) * factor)
-        top_ref[at, :] = jnp.broadcast_to(top, (TILE, width))
-        sum_ref[at, :] = weights[:, :width] + weights[:, width:]
-        acc_ref[at, :] = attend(weights, kv_ref[:, pair:])
-        return carry
-
-    lax.fori_loop(0, tiles, own_tile, 0)
+        ahead = anchor * span + lax.rem(lane, span) - row // heads
+        scores = own_scores(0)
+        for index in range(tiles):
+            following = own_scores(index + 1) if index + 1 < tiles else None
+            q_block = index // (tiles // 2)
+            q_offset = (index - q_block * (tiles // 2)) * TILE // heads
+            allowed = ahead <= span_ref[here + q_block] * span + q_offset
+            scores = jnp.where(allowed, scores, MASKED)
+            top = jnp.max(scores, axis=1, keepdims=True)
+            weights = jnp.exp2((scores - top) * factor)
+            top_ref[at(index), :] = jnp.broadcast_to(top, (TILE, width))
+            sum_ref[at(index), :] = weights[:, :width] + weights[:, width:]
+            acc_ref[at(index), :] = attend(weights, kv_ref[:, pair:])
+            scores = following
+
+    visit_own()
 
     def visit(src_outer, src_inner):
         base = (src_outer * n_inner + src_inner) * 2
         anchors = [span_ref[base], span_ref[base + 1]]
         place = held.at[src_outer, src_inner]
 
-        def tile(index, carry):
-            at = pl.ds(pl.multiple_of(index * TILE, TILE), TILE)
+        def settle_sum(index, rescale, added):
+            acc_ref[at(index), :] = acc_ref[at(index), :] * rescale + added
+
+        scores = scores_of(wide_ref[at(0), :], place[:, :pair])
+        waiting = None
+        for index in range(tiles):
+            following = None
+            if index + 1 < tiles:
+                following = scores_of(wide_ref[at(index + 1), :], place[:, :pair])
             q_anchor = span_ref[here + index // (tiles // 2)]
             bias = [jnp.where(anchor < q_anchor, 0.0, MASKED) for anchor in anchors]
-            scores = scores_of(wide_ref[at, :], place[:, :pair])
             left = scores[:, :width] + bias[0]
             right = scores[:, width:] + bias[1]
-            old = top_ref[at, :]
+            old = top_ref[at(index), :]
             top = jnp.maximum(old, jnp.max(jnp.maximum(left, right), axis=1, keepdims=True))
             rescale = jnp.exp2((old - top) * factor)
             left = jnp.exp2((left - top) * factor)
             right = jnp.exp2((right - top) * factor)
-            top_ref[at, :] = top
-            sum_ref[at, :] = sum_ref[at, :] * rescale + (left + right)
+            top_ref[at(index), :] = top
+            sum_ref[at(index), :] = sum_ref[at(index), :] * rescale + (left + right)
             weights = jnp.concatenate([left, right], axis=1)
-            acc_ref[at, :] = acc_ref[at, :] * rescale + attend(weights, place[:, pair:])
-            return carry
-
-        lax.fori_loop(0, tiles, tile, 0, unroll=2)
+            added = attend(weights, place[:, pair:])
+            if waiting is not None:
+                settle_sum(*waiting)
+            waiting = (index, rescale, added)
+            scores = following
+        settle_sum(*waiting)
 
     below = jnp.minimum(outer, n_outer - 1 - outer)
 
@@ -209,13 +223,9 @@
     lax.fori_loop(1, n_outer, line_step, 0)
     from_inner(nth(n_outer - 1))
 
-    def finish(index, carry):
-        at = pl.ds(pl.multiple_of(index * TILE, TILE), TILE)
-        total = jnp.sum(sum_ref[at, :], axis=1, keepdims=True)
-        o_ref[at, :] = (acc_ref[at, :] / total).astype(o_ref.dtype)
-        return carry
-
-    lax.fori_loop(0, tiles, finish, 0)
+    for index in range(tiles):
+        total = jnp.sum(sum_ref[at(index), :], axis=1, keepdims=True)
+        o_ref[at(index), :] = (acc_ref[at(index), :] / total).astype(o_ref.dtype)
 
     def settle(src_outer, carry):
         for part in range(CHUNKS):

time: 43 us -> 33.7 us (0.78)
  Pallas kernels: 40.3 us -> 31 us
    pallas_call x1, Pallas kernels: 40.3 us -> 31 us  [body(): pl.pallas_call(functools.partial(kernel, n_outer, n_inner, heads), out_sh...]
where the time goes in v1:
time: 33.7 us; the launch traced here: 33.6 us
  Pallas kernels  31 us (92%)
  local copies, waits for them, and re-layouts  2.5 us (7%)
    pallas_call x1, Pallas kernels, body(): pl.pallas_call(functools.partial(kernel, n_outer, n_inner, heads), out_sh...  31 us
    unnamed x5, local copies, waits for them, and re-layouts  1.44 us
    reshape x1, local copies, waits for them, and re-layouts, body(): value.reshape(kv_rows, groups * width)  1.06 us

profile of v1, /device:TPU:0, one launch (start us, length us, event | category | flops | bytes accessed | tf_op | source)
XLA Modules:
  0.0 33.6 jit_solution(11057354318160438358)
XLA Ops:
  0.0 0.0 copy-start
  0.0 1.1 %copy_bitcast_fusion = (bf16[256,256]{1,0:T(8,128)(2,1)S(1)}, bf16[256,256]{1,0:T(8,128)(2,1)S(1)}) fusion(bf16[32,8,2,128]{3,2,1,0:T(2,128)(2,1)} %bitcast.10, bf16[32,8,2,128]{3,2,1,0:T(2,128)(2,1)} %bitcast.11), kind=kLoop, calls=%fused_computation.1 | loop fusion | bytes 524288 | tf_op jit(solution)/shard_map/reshape | solution.py:246
  1.1 0.0 copy-start.1
  1.1 0.1 copy-done
  1.2 0.6 %copy-done.1 = s32[16]{0:T(128)S(1)} copy-done((s32[16]{0:T(128)S(1)}, s32[16]{0:T(128)}, u32[]{:S(2)}) %copy-start.1) | copy-done | bytes 88
  1.7 31.0 %shard_map.46 = bf16[2048,128]{1,0:T(8,128)(2,1)S(1)} custom-call(s32[16]{0:T(128)S(1)} %copy-done.1, bf16[2048,128]{1,0:T(8,128)(2,1)S(1)} %bitcast.9, bf16[256,512]{1,0:T(8,128)(2,1)S(1)} %pad_maximum_fusion.kv_ref), custom_call_target="tpu_custom_call" | custom-call | tf_op jit(solution)/shard_map/pallas_call | solution.py:249
  32.8 0.8 %copy.10 = bf16[256,8,128]{2,1,0:T(8,128)(2,1)} copy(bf16[256,8,128]{2,1,0:T(8,128)(2,1)S(1)} %bitcast.8) | data formatting | bytes 1048576
  (1 shorter events, 0.0 us)
Async XLA Ops:
  0.0 1.2 %copy-start = (bf16[256,8,128]{2,1,0:T(8,128)(2,1)S(1)}, bf16[256,8,128]{2,1,0:T(8,128)(2,1)}, u32[]{:S(2)}) copy-start(bf16[256,8,128]{2,1,0:T(8,128)(2,1)} %param.4) | copy-start | bytes 1572868
  1.1 0.7 %copy-start.1 = (s32[16]{0:T(128)S(1)}, s32[16]{0:T(128)}, u32[]{:S(2)}) copy-start(s32[16]{0:T(128)} %span_ref.1) | copy-start | bytes 196

commit v2 on v1

--- a/solution.py
+++ b/solution.py
@@ -11,17 +11,19 @@
 MESH = pl.DeviceIdType.MESH
 MASKED = -1e30
 TILE = 512
-CHUNKS = 2
+CHUNKS = 4
 
 
 def kernel(
     n_outer,
     n_inner,
     heads,
-    span_ref,
+    span_hbm,
     q_ref,
     kv_ref,
     o_ref,
+    span_ref,
+    span_sem,
     wide_ref,
     held,
     top_ref,
@@ -30,6 +32,7 @@
     send_up,
     send_down,
     send_across,
+    send_buddy,
     recv_sem,
 ):
     rows, width = q_ref.shape
@@ -41,6 +44,11 @@
     factor = math.log2(math.e) / math.sqrt(width)
     outer = lax.axis_index("outer")
     inner = lax.axis_index("inner")
+    use_buddy = n_outer % 2 == 0 and n_outer > 2
+    buddy = outer + 1 - 2 * lax.rem(outer, 2) if use_buddy else n_outer
+
+    spans = pltpu.make_async_copy(span_hbm, span_ref, span_sem)
+    spans.start()
 
     barrier = pltpu.get_barrier_semaphore()
 
@@ -99,8 +107,28 @@
         def _():
             act(down(source, src_outer, part))
 
-        for step in range(1, n_inner):
-            act(across(source, src_outer, part, step))
+        @pl.when(jnp.logical_or(src_outer != buddy, part < CHUNKS // 2))
+        def _():
+            for step in range(1, n_inner):
+                act(across(source, src_outer, part, step))
+
+    def to_buddy(act):
+        def one(step, carry):
+            src_inner = lax.rem(inner + step, n_inner)
+            for part in range(CHUNKS // 2, CHUNKS):
+                act(
+                    copy_of(
+                        held.at[outer, src_inner],
+                        outer,
+                        src_inner,
+                        part,
+                        send_buddy.at[step - 1, part],
+                        {"outer": buddy},
+                    )
+                )
+            return carry
+
+        lax.fori_loop(1, n_inner, one, 0)
 
     def arrived(src_outer, src_inner, part):
         place = held.at[src_outer, src_inner, pl.ds(part * chunk, chunk)]
@@ -115,6 +143,8 @@
 
     for part in range(CHUNKS):
         pass_on(kv_ref, outer, part, lambda copy: copy.start())
+
+    spans.wait()
 
     row_head = lax.rem(lax.broadcasted_iota(jnp.int32, (TILE, width), 0), heads)
     first_head = row_head < heads // 2
@@ -205,23 +235,55 @@
         return jnp.where(upward, outer + distance, outer - distance)
 
     def from_inner(src_outer):
-        for step in range(1, n_inner):
+        def one(step, carry):
             src_inner = lax.rem(inner + step, n_inner)
             for part in range(CHUNKS):
                 arrived(src_outer, src_inner, part)
             visit(src_outer, src_inner)
-
-    def line_step(step, carry):
-        src_outer = nth(step)
-        for part in range(CHUNKS):
+            return carry
+
+        lax.fori_loop(1, n_inner, one, 0)
+
+    def take(src_outer, parts):
+        for part in parts:
             arrived(src_outer, inner, part)
             pass_on(held.at[src_outer, inner], src_outer, part, lambda copy: copy.start())
-        from_inner(nth(step - 1))
-        visit(src_outer, inner)
+
+    def line_step(step, carry):
+        take(nth(step), range(CHUNKS // 2))
+
+        @pl.when(step > 1)
+        def _():
+            visit(nth(step - 1), inner)
+
+        take(nth(step), range(CHUNKS // 2, CHUNKS))
+
+        @pl.when(jnp.logical_and(step > 1, nth(step - 2) != buddy))
+        def _():
+            from_inner(nth(step - 2))
+
         return carry
 
     lax.fori_loop(1, n_outer, line_step, 0)
-    from_inner(nth(n_outer - 1))
+    if use_buddy:
+        to_buddy(lambda copy: copy.start())
+    visit(nth(n_outer - 1), inner)
+
+    def last_step(step, carry):
+        src_outer = jnp.where(step == 0, nth(n_outer - 2), nth(n_outer - 1))
+        if use_buddy:
+            src_outer = jnp.where(step == 1, buddy, src_outer)
+            wanted = jnp.logical_or(step == 1, src_outer != buddy)
+        else:
+            wanted = step != 1
+
+        @pl.when(wanted)
+        def _():
+            from_inner(src_outer)
+
+        return carry
+
+    lax.fori_loop(0, 3, last_step, 0)
 
     for index in range(tiles):
         total = jnp.sum(sum_ref[at(index), :], axis=1, keepdims=True)
@@ -233,6 +295,8 @@
         return carry
 
     lax.fori_loop(0, n_outer, settle, 0)
+    if use_buddy:
+        to_buddy(lambda copy: copy.wait_send())
 
 
 def solution(mesh):
@@ -249,9 +313,11 @@
         out = pl.pallas_call(
             functools.partial(kernel, n_outer, n_inner, heads),
             out_shape=jax.ShapeDtypeStruct((rows, width), jnp.bfloat16),
-            in_specs=[pl.BlockSpec(memory_space=pltpu.SMEM), vmem, vmem],
+            in_specs=[pl.BlockSpec(memory_space=pltpu.HBM), vmem, vmem],
             out_specs=vmem,
             scratch_shapes=[
+                pltpu.SMEM(span_order.shape, jnp.int32),
+                pltpu.SemaphoreType.DMA,
                 pltpu.VMEM((rows, groups * width), jnp.bfloat16),
                 pltpu.VMEM((n_outer, n_inner) + kv.shape, jnp.bfloat16),
                 pltpu.VMEM((rows, width), jnp.float32),
@@ -260,6 +326,7 @@
                 pltpu.SemaphoreType.DMA((n_outer, CHUNKS)),
                 pltpu.SemaphoreType.DMA((n_outer, CHUNKS)),
                 pltpu.SemaphoreType.DMA((n_outer, CHUNKS, max(n_inner - 1, 1))),
+                pltpu.SemaphoreType.DMA((max(n_inner - 1, 1), CHUNKS)),
                 pltpu.SemaphoreType.DMA((n_outer, n_inner, CHUNKS)),
             ],
             compiler_params=pltpu.CompilerParams(

time: 33.7 us -> 32.3 us (0.958)
  Pallas kernels: 31 us -> 29.6 us
    pallas_call x1, Pallas kernels: 31 us -> 29.6 us  [body(): pl.pallas_call(functools.partial(kernel, n_outer, n_inner, heads), out_sh...]
where the time goes in v2:
time: 32.3 us; the launch traced here: 32.2 us
  Pallas kernels  29.6 us (92%)
  local copies, waits for them, and re-layouts  2.5 us (8%)
    pallas_call x1, Pallas kernels, body(): pl.pallas_call(functools.partial(kernel, n_outer, n_inner, heads), out_sh...  29.6 us
    unnamed x5, local copies, waits for them, and re-layouts  1.44 us
    reshape x1, local copies, waits for them, and re-layouts, body(): value.reshape(kv_rows, groups * width)  1.06 us

profile of v2, /device:TPU:0, one launch (start us, length us, event | category | flops | bytes accessed | tf_op | source)
XLA Modules:
  0.0 32.2 jit_solution(6487831396317655409)
XLA Ops:
  0.0 0.0 copy-start
  0.0 1.1 %copy_bitcast_fusion = (bf16[256,256]{1,0:T(8,128)(2,1)S(1)}, bf16[256,256]{1,0:T(8,128)(2,1)S(1)}) fusion(bf16[32,8,2,128]{3,2,1,0:T(2,128)(2,1)} %bitcast.10, bf16[32,8,2,128]{3,2,1,0:T(2,128)(2,1)} %bitcast.11), kind=kLoop, calls=%fused_computation.1 | loop fusion | bytes 524288 | tf_op jit(solution)/shard_map/reshape | solution.py:310
  1.1 0.0 copy-start.1
  1.1 0.1 copy-done
  1.2 0.6 %copy-done.1 = s32[16]{0:T(128)S(1)} copy-done((s32[16]{0:T(128)S(1)}, s32[16]{0:T(128)}, u32[]{:S(2)}) %copy-start.1) | copy-done | bytes 88
  1.7 29.6 %shard_map.46 = bf16[2048,128]{1,0:T(8,128)(2,1)S(1)} custom-call(s32[16]{0:T(128)S(1)} %copy-done.1, bf16[2048,128]{1,0:T(8,128)(2,1)S(1)} %bitcast.9, bf16[256,512]{1,0:T(8,128)(2,1)S(1)} %pad_maximum_fusion.kv_ref), custom_call_target="tpu_custom_call" | custom-call | tf_op jit(solution)/shard_map/pallas_call | solution.py:313
  31.4 0.8 %copy.10 = bf16[256,8,128]{2,1,0:T(8,128)(2,1)} copy(bf16[256,8,128]{2,1,0:T(8,128)(2,1)S(1)} %bitcast.8) | data formatting | bytes 1048576
  (1 shorter events, 0.0 us)
Async XLA Ops:
  0.0 1.2 %copy-start = (bf16[256,8,128]{2,1,0:T(8,128)(2,1)S(1)}, bf16[256,8,128]{2,1,0:T(8,128)(2,1)}, u32[]{:S(2)}) copy-start(bf16[256,8,128]{2,1,0:T(8,128)(2,1)} %param.4) | copy-start | bytes 1572868
  1.1 0.7 %copy-start.1 = (s32[16]{0:T(128)S(1)}, s32[16]{0:T(128)}, u32[]{:S(2)}) copy-start(s32[16]{0:T(128)} %span_hbm.1) | copy-start | bytes 196
